TPU v7x, 32 devices: a whole 2x2x4 slice. The times are simulated.
32 devices in a mesh: robot: 8 (over z, x), sub: 4 (over y, core).
Axes of the slice: x: 2, y: 2, z: 4, core: 2. Of those that a mesh axis runs over, the one named last changes fastest.
Arguments:
- landmark_copies: float32 [8, 4, 3, 512], P('robot', 'sub'), may hold values from -6 to 6
- dual_copies: float32 [8, 4, 3, 512], P('robot', 'sub'), may hold values from -4 to 4
- visibility: int32 [8, 4, 512], P('robot', 'sub'), may hold values from 0 to 511
- block_counts: int32 [8, 4, 8], P('robot', 'sub'), may hold values from 1 to 64, as said below
- consensus_old: float32 [8, 4, 3, 512], P('robot', 'sub'), may hold values from -6 to 6
- poses: float32 [8, 4, 6, 1024], P('robot', 'sub'), may hold values from -6 to 6
- inverse_blocks: float32 [8, 4, 36, 1024], P('robot', 'sub'), may hold values from -1.8 to 1.8
- jacobians: float32 [8, 4, 18, 4096], P('robot', 'sub'), may hold values from -3 to 3
- measurements: float32 [8, 4, 3, 4096], P('robot', 'sub'), may hold values from -6 to 6
- obs_pose: int32 [8, 4, 4096], P('robot', 'sub'), may hold values from 0 to 1023
- obs_slot: int32 [8, 4, 4096], P('robot', 'sub'), may hold values from 0 to 511, as said below
- edge_to: int32 [8, 4, 1024], P('robot', 'sub'), may hold values from 0 to 4095
- edge_offset: float32 [8, 4, 6, 1024], P('robot', 'sub'), may hold values from -3 to 3
Outputs:
- refined_poses: float32 [8, 4, 6, 1024], P('robot', 'sub')
- consensus: float32 [8, 4, 3, 512], P('robot', 'sub')
- dual_new: float32 [8, 4, 3, 512], P('robot', 'sub')
- residual_norms: float32 [2], replicated
Inputs may be any that keep to these rules, and one draw needn't show every extreme that they name: block_counts[r,s,d] counts the live slots at the head of block d; for every sub index some robot receives full blocks from every robot, which robot varies with the draw. `obs_slot`: each observation names a live slot of its own device.
All inputs are finite; a program needn't handle non-finite values.
Results may differ from a plain program's by a relative error of at most 0.0001.
Values sent between devices are 32-bit elements; how exact they have to be, the bound alone decides.
No kernel may reach another device: no remote copies, remote signals or barrier semaphores. Data moves between devices by JAX's collectives and lax.ppermute only.
A program may use at most 64 MiB of HBM per device.

v0:
```python
import jax
import jax.numpy as jnp
from jax import lax
from jax.sharding import PartitionSpec as P

penalty = 2.0


def body(
    landmark_copies,
    dual_copies,
    visibility,
    block_counts,
    consensus_old,
    poses,
    inverse_blocks,
    jacobians,
    measurements,
    obs_pose,
    obs_slot,
    edge_to,
    edge_offset,
):
    copies = landmark_copies[0, 0]
    duals = dual_copies[0, 0]
    slot_ids = visibility[0]
    counts = block_counts[0, 0]
    old_estimate = consensus_old[0, 0]
    robots = lax.axis_size("robot")
    slot_count = copies.shape[1]
    block_size = slot_count // robots
    owned = old_estimate.shape[1]
    live_mask = (
        (jnp.arange(block_size)[None, :] < counts[:, None]).reshape(slot_count).astype(jnp.float32)
    )
    outgoing = jnp.concatenate([(copies + duals) * live_mask[None, :], live_mask[None, :]], axis=0)
    received, received_ids = (
        lax.all_to_all(outgoing, "robot", split_axis=1, concat_axis=1, tiled=True),
        lax.all_to_all(slot_ids, "robot", split_axis=1, concat_axis=1, tiled=True),
    )
    owner_ids = received_ids[0]
    totals = jax.vmap(lambda entries: jax.ops.segment_sum(entries, owner_ids, num_segments=owned))(
        received
    )
    consensus = (old_estimate + totals[:3]) / (1.0 + totals[3:4])
    returning = consensus[:, owner_ids]
    back = lax.all_to_all(returning, "robot", split_axis=1, concat_axis=1, tiled=True)
    differ = (copies - back) * live_mask[None, :]
    dual_new = duals + differ
    primal = jnp.sum(differ * differ)
    change = consensus - old_estimate
    dualsum = penalty * penalty * jnp.sum(totals[3:4] * change * change)
    primal_all, dual_all = lax.psum((primal, dualsum), ("robot", "sub"))
    landmark_total = owned * robots * lax.axis_size("sub")
    residual_norms = jnp.sqrt(jnp.stack([primal_all, dual_all]) / landmark_total)
    pose_block = poses[0, 0]
    pose_count = pose_block.shape[1]
    robot_all = lax.all_gather(pose_block, "sub", axis=1, tiled=True)
    pose_far = robot_all[:, edge_to[0, 0]]
    copies_at = copies[:, obs_slot[0, 0]]
    error = measurements[0, 0] - copies_at
    jac_rows = jacobians[0, 0].reshape(3, 6, error.shape[1])
    pull = jnp.sum(jac_rows * error[:, None, :], axis=0)
    pose_ids = obs_pose[0, 0]
    grad_obs = jax.vmap(
        lambda entries: jax.ops.segment_sum(entries, pose_ids, num_segments=pose_count)
    )(pull)
    grad = grad_obs + pose_far - pose_block - edge_offset[0, 0]
    inverse = inverse_blocks[0, 0].reshape(6, 6, pose_count)
    delta = jnp.sum(inverse * grad[None, :, :], axis=1)
    refined = pose_block + delta
    return (refined[None, None], consensus[None, None], dual_new[None, None], residual_norms)


def solution(mesh):
    return jax.shard_map(
        body,
        mesh=mesh,
        in_specs=(
            P("robot", "sub", None, None),
            P("robot", "sub", None, None),
            P("robot", "sub", None),
            P("robot", "sub", None),
            P("robot", "sub", None, None),
            P("robot", "sub", None, None),
            P("robot", "sub", None, None),
            P("robot", "sub", None, None),
            P("robot", "sub", None, None),
            P("robot", "sub", None),
            P("robot", "sub", None),
            P("robot", "sub", None),
            P("robot", "sub", None, None),
        ),
        out_specs=(
            P("robot", "sub", None, None),
            P("robot", "sub", None, None),
            P("robot", "sub", None, None),
            P(),
        ),
        check_vma=False,
    )
```

profile of v0, /device:TPU:0, one launch (start us, length us, event | category | flops | bytes accessed | tf_op | source)
XLA Modules:
  0.0 154.9 jit_solution(5562532823633209940)
XLA Ops:
  1.1 1.3 reduce.16
  3.2 7.3 %all-to-all-start = ((s32[1,8,64]{2,0,1:T(1,128)}), s32[1,8,64]{2,0,1:T(1,128)S(1)}, u32[]{:S(2)}, u32[]{:S(2)}) async-start(s32[1,8,64]{2,0,1:T(1,128)} %all_to_all.22), calls=%async_computation | async-start | bytes 8192 | tf_op jit(solution)/shard_map/all_to_all | solution.py:39
  11.9 0.8 copy.53
  12.7 0.7 add_reduce_fusion.1
  13.6 0.7 compare_select_fusion
  14.3 1.4 copy.52
  15.7 14.1 %gather_fusion.1 = f32[4096,3]{1,0:T(8,128)} fusion(f32[3,512]{0,1:T(8,128)S(1)} %bitcast.54, s32[4096]{0:T(1024)S(1)} %broadcast_clamp_fusion), kind=kCustom, calls=%fused_computation.1 | custom fusion | bytes 114688 | tf_op jit(solution)/shard_map/gather | solution.py:60
  29.8 3.2 %bitcast_subtract_fusion = f32[3,4096]{0,1:T(8,128)} fusion(f32[4096,3]{1,0:T(8,128)} %gather_fusion.1, f32[1,1,3,4096]{2,3,1,0:T(8,128)S(1)} %copy.52), kind=kLoop, calls=%fused_computation.5 | loop fusion | flops 12288 | bytes 147456 | tf_op jit(solution)/shard_map/sub | solution.py:61
  33.0 2.3 %copy.54 = f32[3,4096]{1,0:T(4,128)S(1)} copy(f32[3,4096]{0,1:T(8,128)} %bitcast_subtract_fusion) | data formatting | bytes 98304 | tf_op jit(solution)/shard_map/sub | solution.py:61
  36.1 2.0 %copy.55 = f32[4096,6]{1,0:T(8,128)} copy(f32[4096,6]{0,1:T(8,128)S(1)} %bitcast.57) | data formatting | bytes 196608 | tf_op jit(solution)/shard_map/reduce_sum | solution.py:63
  38.3 15.8 %all-gather = f32[1,1,6,4096]{2,3,1,0:T(8,128)S(1)} all-gather(f32[1,1,6,1024]{2,3,1,0:T(8,128)S(1)} %copy.51), channel_id=2, replica_groups=mesh['robot'=8,'sub'=4] {'sub'}, dimensions={3}, use_global_device_ids=true | all-gather | bytes 122880 | tf_op jit(solution)/shard_map/all_gather | solution.py:58
  54.1 1.0 copy.57
  55.1 2.8 %gather_fusion = f32[1024,6]{1,0:T(8,128)S(1)} fusion(f32[6,4096]{0,1:T(8,128)S(1)} %bitcast.55, s32[1024]{0:T(1024)S(1)} %broadcast_clamp_fusion.1), kind=kCustom, calls=%fused_computation | custom fusion | bytes 53248 | tf_op jit(solution)/shard_map/gather | solution.py:59
  58.0 22.9 %scatter_fusion = f32[6,1024]{0,1:T(8,128)S(1)} fusion(f32[6,1024]{0,1:T(8,128)S(1)} %bitcast.53, s32[4096]{0:T(1024)S(1)} %bitcast.67, f32[4096,6]{1,0:T(8,128)} %copy.55), kind=kCustom, calls=%fused_computation.3 | custom fusion | flops 24576 | bytes 311296 | tf_op jit(solution)/shard_map/vmap()/scatter-add | solution.py:66
  82.6 6.0 %all-to-all-start.1 = ((f32[8,1,256]{2,1,0:T(1,128)}), f32[8,1,256]{2,1,0:T(1,128)S(1)}, u32[]{:S(2)}, u32[]{:S(2)}) async-start(f32[8,1,256]{2,1,0:T(1,128)} %reshape.262), calls=%async_computation.1 | async-start | bytes 16384 | tf_op jit(solution)/shard_map/all_to_all | solution.py:38
  89.4 5.7 %all-to-all-done.1 = f32[8,1,256]{2,1,0:T(1,128)S(1)} async-done(((f32[8,1,256]{2,1,0:T(1,128)}), f32[8,1,256]{2,1,0:T(1,128)S(1)}, u32[]{:S(2)}, u32[]{:S(2)}) %all-to-all-start.1) | async-done | bytes 8224 | tf_op jit(solution)/shard_map/all_to_all | solution.py:38
  96.6 2.3 %scatter_custom_fusion.1 = f32[4,512]{0,1:T(8,128)S(1)} fusion(s32[512]{0:T(512)S(1)} %reshape.227, f32[512,4]{1,0:T(8,128)S(1)} %copy.62, f32[]{:T(128)} %constant.10.clone.1), kind=kCustom, calls=%fused_computation.21 | custom fusion | flops 2048 | bytes 8196 | tf_op jit(solution)/shard_map/vmap()/scatter-add | solution.py:42
  99.2 0.8 fusion
  100.0 1.0 gather_fusion.2
  101.9 3.3 %all-to-all-start.2 = ((f32[8,1,192]{2,1,0:T(1,128)}), f32[8,1,192]{2,1,0:T(1,128)S(1)}, u32[]{:S(2)}, u32[]{:S(2)}) async-start(f32[8,1,192]{2,1,0:T(1,128)} %reshape.264), calls=%async_computation.2 | async-start | bytes 16384 | tf_op jit(solution)/shard_map/all_to_all | solution.py:47
  107.3 4.4 %all-to-all-done.2 = f32[8,1,192]{2,1,0:T(1,128)S(1)} async-done(((f32[8,1,192]{2,1,0:T(1,128)}), f32[8,1,192]{2,1,0:T(1,128)S(1)}, u32[]{:S(2)}, u32[]{:S(2)}) %all-to-all-start.2) | async-done | bytes 6176 | tf_op jit(solution)/shard_map/all_to_all | solution.py:47
  112.7 0.7 fusion.4
  114.1 38.9 %all-reduce = (f32[1]{0:T(128)}, f32[1]{0:T(128)}) all-reduce(f32[1]{0:T(128)} %bitcast.22, f32[1]{0:T(128)} %bitcast.21), channel_id=1, replica_groups=mesh['robot'=8,'sub'=4] {'robot','sub'}, use_global_device_ids=true, to_apply=%region_7.0 | all-reduce | flops 2 | bytes 16 | tf_op jit(solution)/shard_map/psum | solution.py:53
  153.0 1.9 %fusion.10 = f32[2]{0:T(128)} fusion(f32[1]{0:T(128)} %get-tuple-element.22, f32[1]{0:T(128)} %get-tuple-element.23), kind=kLoop, calls=%fused_computation.41 | loop fusion | flops 4 | bytes 16 | tf_op jit(solution)/shard_map/sqrt | solution.py:55
  (67 shorter events, 11.8 us)
Async XLA Ops:
  3.2 79.4 %all-to-all-start = ((s32[1,8,64]{2,0,1:T(1,128)}), s32[1,8,64]{2,0,1:T(1,128)S(1)}, u32[]{:S(2)}, u32[]{:S(2)}) async-start(s32[1,8,64]{2,0,1:T(1,128)} %all_to_all.22), calls=%async_computation | async-start | bytes 8192 | tf_op jit(solution)/shard_map/all_to_all | solution.py:39
  33.0 2.3 %copy-start.1 = (f32[1,1,18,4096]{3,1,2,0:T(1,128)S(1)}, f32[1,1,18,4096]{3,1,2,0:T(1,128)}, u32[]{:S(2)}) copy-start(f32[1,1,18,4096]{3,1,2,0:T(1,128)} %param.20) | copy-start | bytes 884740
  35.2 2.8 %copy-start.3 = (f32[1,1,6,1024]{3,1,2,0:T(1,128)S(1)}, f32[1,1,6,1024]{3,1,2,0:T(1,128)}, u32[]{:S(2)}) copy-start(f32[1,1,6,1024]{3,1,2,0:T(1,128)} %param.18) | copy-start | bytes 73732
  38.1 16.0 %copy-start.9 = (s32[1,1,1024]{2,1,0:T(1,128)S(1)}, s32[1,1,1024]{2,1,0:T(1,128)}, u32[]{:S(2)}) copy-start(s32[1,1,1024]{2,1,0:T(1,128)} %param.24) | copy-start | bytes 12292
  38.1 16.0 %copy-start.5 = (f32[1,1,6,1024]{3,1,2,0:T(1,128)S(1)}, f32[1,1,6,1024]{3,1,2,0:T(1,128)}, u32[]{:S(2)}) copy-start(f32[1,1,6,1024]{3,1,2,0:T(1,128)} %param.25) | copy-start | bytes 73732
  38.1 19.9 %copy-start.7 = (s32[1,1,4096]{2,1,0:T(1,128)S(1)}, s32[1,1,4096]{2,1,0:T(1,128)}, u32[]{:S(2)}) copy-start(s32[1,1,4096]{2,1,0:T(1,128)} %param.22) | copy-start | bytes 49156
  57.9 23.0 %copy-start = (f32[1,1,6,1024]{2,3,1,0:T(8,128)S(1)}, f32[1,1,6,1024]{2,3,1,0:T(8,128)}, u32[]{:S(2)}) copy-start(f32[1,1,6,1024]{2,3,1,0:T(8,128)} %copy.57) | copy-start | bytes 73732
  58.0 23.2 %copy-start.2 = (f32[1,1,36,1024]{3,1,2,0:T(1,128)S(1)}, f32[1,1,36,1024]{3,1,2,0:T(1,128)}, u32[]{:S(2)}) copy-start(f32[1,1,36,1024]{3,1,2,0:T(1,128)} %param.19) | copy-start | bytes 442372
  80.9 1.5 copy-start.8
  81.6 31.9 %copy-start.4 = (f32[1,1,3,512]{3,1,2,0:T(1,128)S(1)}, f32[1,1,3,512]{3,1,2,0:T(1,128)}, u32[]{:S(2)}) copy-start(f32[1,1,3,512]{3,1,2,0:T(1,128)} %param.13) | copy-start | bytes 18436
  81.6 31.9 %copy-start.6 = (f32[1,1,3,512]{3,1,2,0:T(1,128)S(1)}, f32[1,1,3,512]{3,1,2,0:T(1,128)}, u32[]{:S(2)}) copy-start(f32[1,1,3,512]{3,1,2,0:T(1,128)} %param.14) | copy-start | bytes 18436
  82.6 12.5 %all-to-all-start.1 = ((f32[8,1,256]{2,1,0:T(1,128)}), f32[8,1,256]{2,1,0:T(1,128)S(1)}, u32[]{:S(2)}, u32[]{:S(2)}) async-start(f32[8,1,256]{2,1,0:T(1,128)} %reshape.262), calls=%async_computation.1 | async-start | bytes 16384 | tf_op jit(solution)/shard_map/all_to_all | solution.py:38
  101.9 9.8 %all-to-all-start.2 = ((f32[8,1,192]{2,1,0:T(1,128)}), f32[8,1,192]{2,1,0:T(1,128)S(1)}, u32[]{:S(2)}, u32[]{:S(2)}) async-start(f32[8,1,192]{2,1,0:T(1,128)} %reshape.264), calls=%async_computation.2 | async-start | bytes 16384 | tf_op jit(solution)/shard_map/all_to_all | solution.py:47
where the time goes:
time: 156 us; the launch traced here: 155 us
  blocking collectives  54.7 us (35%)
  other arithmetic  40.4 us (26%)
  local copies, waits for them, and re-layouts  31.6 us (20%)
  starting transfers between devices  16.6 us (11%)
  waiting for transfers between devices  10.1 us (6%)
  between operations  1.6 us (1%)
    psum x1, blocking collectives, body(): primal_all, dual_all = lax.psum((primal, dualsum), ('robot', 'sub'))  38.9 us
    scatter-add x1, other arithmetic, body(): jax.ops.segment_sum(entries, pose_ids, num_segments=pose_count)  22.9 us
    all_gather x1, blocking collectives, body(): robot_all = lax.all_gather(pose_block, 'sub', axis=1, tiled=True)  15.8 us
    gather x1, local copies, waits for them, and re-layouts, body(): copies_at = copies[:, obs_slot[0, 0]]  14.1 us
    all_to_all x1, starting transfers between devices, body(): lax.all_to_all(slot_ids, 'robot', split_axis=1, concat_axis=1, tiled=True)  7.28 us
    unnamed x32, local copies, waits for them, and re-layouts  7.06 us
    all_to_all x1, starting transfers between devices, body(): lax.all_to_all(outgoing, 'robot', split_axis=1, concat_axis=1, tiled=True)  6.01 us
    all_to_all x1, waiting for transfers between devices, body(): lax.all_to_all(outgoing, 'robot', split_axis=1, concat_axis=1, tiled=True)  5.69 us
  transfers between devices with their start and end apart: 3, of which 2 were waited for; matrix products, arithmetic and copies ran while one was open for 38% of the time, Pallas kernels for 0%

commit v1 on v0

--- a/solution.py
+++ b/solution.py
@@ -4,6 +4,7 @@
 from jax.sharding import PartitionSpec as P
 
 penalty = 2.0
+store_routes_all = lambda in_array: lax.psum(lax.psum(in_array, "sub"), "robot")
 
 
 def body(
@@ -50,7 +51,7 @@
     primal = jnp.sum(differ * differ)
     change = consensus - old_estimate
     dualsum = penalty * penalty * jnp.sum(totals[3:4] * change * change)
-    primal_all, dual_all = lax.psum((primal, dualsum), ("robot", "sub"))
+    primal_all, dual_all = store_routes_all((primal, dualsum))
     landmark_total = owned * robots * lax.axis_size("sub")
     residual_norms = jnp.sqrt(jnp.stack([primal_all, dual_all]) / landmark_total)
     pose_block = poses[0, 0]

time: 156 us -> 141 us (0.904)
  blocking collectives: 54.7 us -> 40.7 us
    psum x1 -> x2, blocking collectives: 38.9 us -> 24.9 us  [the longest x1 18.3 us: lax.psum(lax.psum(in_array, 'sub'), 'robot')]
  transfers between devices with their start and end apart: 3 -> 3, of which waited for: 2 -> 2; matrix products, arithmetic and copies ran while one was open for 38% -> 41% of each run, Pallas kernels for 0% -> 0%
where the time goes in v1:
time: 141 us
  blocking collectives  40.7 us (29%)
  other arithmetic  40.2 us (29%)
  local copies, waits for them, and re-layouts  31.6 us (22%)
  starting transfers between devices  16.6 us (12%)
  waiting for transfers between devices  10.1 us (7%)
  between operations  1.6 us (1%)
    scatter-add x1, other arithmetic, body(): jax.ops.segment_sum(entries, pose_ids, num_segments=pose_count)  22.9 us
    psum x1, blocking collectives, lax.psum(lax.psum(in_array, 'sub'), 'robot')  18.3 us
    all_gather x1, blocking collectives, body(): robot_all = lax.all_gather(pose_block, 'sub', axis=1, tiled=True)  15.8 us
    gather x1, local copies, waits for them, and re-layouts, body(): copies_at = copies[:, obs_slot[0, 0]]  14.1 us
    all_to_all x1, starting transfers between devices, body(): lax.all_to_all(slot_ids, 'robot', split_axis=1, concat_axis=1, tiled=True)  7.28 us
    unnamed x32, local copies, waits for them, and re-layouts  7.06 us
    psum x1, blocking collectives, lax.psum(in_array, 'sub')  6.59 us
    all_to_all x1, starting transfers between devices, body(): lax.all_to_all(outgoing, 'robot', split_axis=1, concat_axis=1, tiled=True)  6.01 us
  transfers between devices with their start and end apart: 3, of which 2 were waited for; matrix products, arithmetic and copies ran while one was open for 41% of the time, Pallas kernels for 0%

profile of v1, /device:TPU:0, one launch (start us, length us, event | category | flops | bytes accessed | tf_op | source)
XLA Modules:
  0.0 140.8 jit_solution(10189685594831924668)
XLA Ops:
  1.1 1.3 reduce.16
  3.2 7.3 %all-to-all-start = ((s32[1,8,64]{2,0,1:T(1,128)}), s32[1,8,64]{2,0,1:T(1,128)S(1)}, u32[]{:S(2)}, u32[]{:S(2)}) async-start(s32[1,8,64]{2,0,1:T(1,128)} %all_to_all.22), calls=%async_computation | async-start | bytes 8192 | tf_op jit(solution)/shard_map/all_to_all | solution.py:40
  11.9 0.8 copy.53
  12.7 0.7 add_reduce_fusion.1
  14.3 1.4 %copy.52 = f32[1,1,3,4096]{2,3,1,0:T(8,128)S(1)} copy(f32[1,1,3,4096]{3,1,2,0:T(1,128)} %param.21) | data formatting | bytes 98304 | tf_op args[8]
  15.7 14.1 %gather_fusion.1 = f32[4096,3]{1,0:T(8,128)} fusion(f32[3,512]{0,1:T(8,128)S(1)} %bitcast.54, s32[4096]{0:T(1024)S(1)} %broadcast_clamp_fusion), kind=kCustom, calls=%fused_computation.1 | custom fusion | bytes 114688 | tf_op jit(solution)/shard_map/gather | solution.py:61
  29.8 3.2 %bitcast_subtract_fusion = f32[3,4096]{0,1:T(8,128)} fusion(f32[4096,3]{1,0:T(8,128)} %gather_fusion.1, f32[1,1,3,4096]{2,3,1,0:T(8,128)S(1)} %copy.52), kind=kLoop, calls=%fused_computation.5 | loop fusion | flops 12288 | bytes 147456 | tf_op jit(solution)/shard_map/sub | solution.py:62
  33.0 2.3 %copy.54 = f32[3,4096]{1,0:T(4,128)S(1)} copy(f32[3,4096]{0,1:T(8,128)} %bitcast_subtract_fusion) | data formatting | bytes 98304 | tf_op jit(solution)/shard_map/sub | solution.py:62
  36.1 2.0 %copy.55 = f32[4096,6]{1,0:T(8,128)} copy(f32[4096,6]{0,1:T(8,128)S(1)} %bitcast.57) | data formatting | bytes 196608 | tf_op jit(solution)/shard_map/reduce_sum | solution.py:64
  38.3 15.8 %all-gather = f32[1,1,6,4096]{2,3,1,0:T(8,128)S(1)} all-gather(f32[1,1,6,1024]{2,3,1,0:T(8,128)S(1)} %copy.51), channel_id=2, replica_groups=mesh['robot'=8,'sub'=4] {'sub'}, dimensions={3}, use_global_device_ids=true | all-gather | bytes 122880 | tf_op jit(solution)/shard_map/all_gather | solution.py:59
  54.1 1.0 copy.57
  55.1 2.8 %gather_fusion = f32[1024,6]{1,0:T(8,128)S(1)} fusion(f32[6,4096]{0,1:T(8,128)S(1)} %bitcast.55, s32[1024]{0:T(1024)S(1)} %broadcast_clamp_fusion.1), kind=kCustom, calls=%fused_computation | custom fusion | bytes 53248 | tf_op jit(solution)/shard_map/gather | solution.py:60
  58.0 22.9 %scatter_fusion = f32[6,1024]{0,1:T(8,128)S(1)} fusion(f32[6,1024]{0,1:T(8,128)S(1)} %bitcast.53, s32[4096]{0:T(1024)S(1)} %bitcast.67, f32[4096,6]{1,0:T(8,128)} %copy.55), kind=kCustom, calls=%fused_computation.3 | custom fusion | flops 24576 | bytes 311296 | tf_op jit(solution)/shard_map/vmap()/scatter-add | solution.py:67
  82.6 6.0 %all-to-all-start.1 = ((f32[8,1,256]{2,1,0:T(1,128)}), f32[8,1,256]{2,1,0:T(1,128)S(1)}, u32[]{:S(2)}, u32[]{:S(2)}) async-start(f32[8,1,256]{2,1,0:T(1,128)} %reshape.262), calls=%async_computation.1 | async-start | bytes 16384 | tf_op jit(solution)/shard_map/all_to_all | solution.py:39
  89.4 5.7 %all-to-all-done.1 = f32[8,1,256]{2,1,0:T(1,128)S(1)} async-done(((f32[8,1,256]{2,1,0:T(1,128)}), f32[8,1,256]{2,1,0:T(1,128)S(1)}, u32[]{:S(2)}, u32[]{:S(2)}) %all-to-all-start.1) | async-done | bytes 8224 | tf_op jit(solution)/shard_map/all_to_all | solution.py:39
  96.6 2.3 %scatter_custom_fusion.1 = f32[4,512]{0,1:T(8,128)S(1)} fusion(s32[512]{0:T(512)S(1)} %reshape.227, f32[512,4]{1,0:T(8,128)S(1)} %copy.62, f32[]{:T(128)} %constant.10.clone.1), kind=kCustom, calls=%fused_computation.21 | custom fusion | flops 2048 | bytes 8196 | tf_op jit(solution)/shard_map/vmap()/scatter-add | solution.py:43
  99.2 0.8 fusion
  100.0 1.0 gather_fusion.2
  101.9 3.3 %all-to-all-start.2 = ((f32[8,1,192]{2,1,0:T(1,128)}), f32[8,1,192]{2,1,0:T(1,128)S(1)}, u32[]{:S(2)}, u32[]{:S(2)}) async-start(f32[8,1,192]{2,1,0:T(1,128)} %reshape.264), calls=%async_computation.2 | async-start | bytes 16384 | tf_op jit(solution)/shard_map/all_to_all | solution.py:48
  107.3 4.4 %all-to-all-done.2 = f32[8,1,192]{2,1,0:T(1,128)S(1)} async-done(((f32[8,1,192]{2,1,0:T(1,128)}), f32[8,1,192]{2,1,0:T(1,128)S(1)}, u32[]{:S(2)}, u32[]{:S(2)}) %all-to-all-start.2) | async-done | bytes 6176 | tf_op jit(solution)/shard_map/all_to_all | solution.py:48
  112.7 0.7 fusion.4
  114.1 6.6 %all-reduce.1 = (f32[]{:T(128)}, f32[]{:T(128)}) all-reduce(f32[]{:T(128)S(6)} %mul_shard_map.3, f32[]{:T(128)} %fusion.4), channel_id=1, replica_groups=mesh['robot'=8,'sub'=4] {'sub'}, use_global_device_ids=true, to_apply=%region_8.0 | all-reduce | flops 2 | bytes 16 | tf_op jit(solution)/shard_map/psum | solution.py:7
  120.7 18.3 %all-reduce = (f32[1]{0:T(128)}, f32[1]{0:T(128)}) all-reduce(f32[1]{0:T(128)} %bitcast.22, f32[1]{0:T(128)} %bitcast.21), channel_id=1, replica_groups=mesh['robot'=8,'sub'=4] {'robot'}, use_global_device_ids=true, to_apply=%region_9.0 | all-reduce | flops 2 | bytes 16 | tf_op jit(solution)/shard_map/psum | solution.py:7
  139.0 1.8 %fusion.10 = f32[2]{0:T(128)} fusion(f32[1]{0:T(128)} %get-tuple-element.22, f32[1]{0:T(128)} %get-tuple-element.23), kind=kLoop, calls=%fused_computation.41 | loop fusion | flops 4 | bytes 16 | tf_op jit(solution)/shard_map/sqrt | solution.py:56
  (68 shorter events, 12.6 us)
Async XLA Ops:
  3.2 79.4 %all-to-all-start = ((s32[1,8,64]{2,0,1:T(1,128)}), s32[1,8,64]{2,0,1:T(1,128)S(1)}, u32[]{:S(2)}, u32[]{:S(2)}) async-start(s32[1,8,64]{2,0,1:T(1,128)} %all_to_all.22), calls=%async_computation | async-start | bytes 8192 | tf_op jit(solution)/shard_map/all_to_all | solution.py:40
  33.0 2.3 %copy-start.1 = (f32[1,1,18,4096]{3,1,2,0:T(1,128)S(1)}, f32[1,1,18,4096]{3,1,2,0:T(1,128)}, u32[]{:S(2)}) copy-start(f32[1,1,18,4096]{3,1,2,0:T(1,128)} %param.20) | copy-start | bytes 884740
  35.2 2.8 %copy-start.3 = (f32[1,1,6,1024]{3,1,2,0:T(1,128)S(1)}, f32[1,1,6,1024]{3,1,2,0:T(1,128)}, u32[]{:S(2)}) copy-start(f32[1,1,6,1024]{3,1,2,0:T(1,128)} %param.18) | copy-start | bytes 73732
  38.1 16.0 %copy-start.9 = (s32[1,1,1024]{2,1,0:T(1,128)S(1)}, s32[1,1,1024]{2,1,0:T(1,128)}, u32[]{:S(2)}) copy-start(s32[1,1,1024]{2,1,0:T(1,128)} %param.24) | copy-start | bytes 12292
  38.1 16.0 %copy-start.5 = (f32[1,1,6,1024]{3,1,2,0:T(1,128)S(1)}, f32[1,1,6,1024]{3,1,2,0:T(1,128)}, u32[]{:S(2)}) copy-start(f32[1,1,6,1024]{3,1,2,0:T(1,128)} %param.25) | copy-start | bytes 73732
  38.1 19.9 %copy-start.7 = (s32[1,1,4096]{2,1,0:T(1,128)S(1)}, s32[1,1,4096]{2,1,0:T(1,128)}, u32[]{:S(2)}) copy-start(s32[1,1,4096]{2,1,0:T(1,128)} %param.22) | copy-start | bytes 49156
  57.9 23.0 %copy-start = (f32[1,1,6,1024]{2,3,1,0:T(8,128)S(1)}, f32[1,1,6,1024]{2,3,1,0:T(8,128)}, u32[]{:S(2)}) copy-start(f32[1,1,6,1024]{2,3,1,0:T(8,128)} %copy.57) | copy-start | bytes 73732
  58.0 23.2 %copy-start.2 = (f32[1,1,36,1024]{3,1,2,0:T(1,128)S(1)}, f32[1,1,36,1024]{3,1,2,0:T(1,128)}, u32[]{:S(2)}) copy-start(f32[1,1,36,1024]{3,1,2,0:T(1,128)} %param.19) | copy-start | bytes 442372
  80.9 1.5 %copy-start.8 = (f32[1,1,3,512]{3,1,2,0:T(1,128)S(1)}, f32[1,1,3,512]{3,1,2,0:T(1,128)}, u32[]{:S(2)}) copy-start(f32[1,1,3,512]{3,1,2,0:T(1,128)} %param.17) | copy-start | bytes 18436
  81.6 31.9 %copy-start.4 = (f32[1,1,3,512]{3,1,2,0:T(1,128)S(1)}, f32[1,1,3,512]{3,1,2,0:T(1,128)}, u32[]{:S(2)}) copy-start(f32[1,1,3,512]{3,1,2,0:T(1,128)} %param.13) | copy-start | bytes 18436
  81.6 31.9 %copy-start.6 = (f32[1,1,3,512]{3,1,2,0:T(1,128)S(1)}, f32[1,1,3,512]{3,1,2,0:T(1,128)}, u32[]{:S(2)}) copy-start(f32[1,1,3,512]{3,1,2,0:T(1,128)} %param.14) | copy-start | bytes 18436
  82.6 12.5 %all-to-all-start.1 = ((f32[8,1,256]{2,1,0:T(1,128)}), f32[8,1,256]{2,1,0:T(1,128)S(1)}, u32[]{:S(2)}, u32[]{:S(2)}) async-start(f32[8,1,256]{2,1,0:T(1,128)} %reshape.262), calls=%async_computation.1 | async-start | bytes 16384 | tf_op jit(solution)/shard_map/all_to_all | solution.py:39
  101.9 9.8 %all-to-all-start.2 = ((f32[8,1,192]{2,1,0:T(1,128)}), f32[8,1,192]{2,1,0:T(1,128)S(1)}, u32[]{:S(2)}, u32[]{:S(2)}) async-start(f32[8,1,192]{2,1,0:T(1,128)} %reshape.264), calls=%async_computation.2 | async-start | bytes 16384 | tf_op jit(solution)/shard_map/all_to_all | solution.py:48
